TPU v7x, 256 devices: a whole 4x4x8 slice. The times are simulated.
256 devices in a mesh: wrow: 32 (over y, x, z_lo), kblk: 8 (over z_hi, core).
Axes of the slice: x: 4, y: 4, z: 8 (z_hi: 4, z_lo: 2; z = z_hi * 2 + z_lo), core: 2. Of those that a mesh axis runs over, the one named last changes fastest.
Arguments:
- conduction: bfloat16 [8, 4, 64, 16384], P('kblk', None, None, 'wrow'), may hold values from -6 to 6
- valence: bfloat16 [8, 4, 64, 16384], P(None, None, 'wrow', 'kblk'), may hold values from -6 to 6
- screened: bfloat16 [4, 16384, 16384], P(None, 'wrow', 'kblk'), may hold values from -0.00036621094 to 0.00036621094
- pair_block: int32 [8, 4], replicated, may hold values from 0 to 3, as said below
Outputs:
- kernel: float32 [8, 64, 256], P('kblk', 'wrow')
Inputs may be any that keep to these rules, and one draw needn't show every extreme that they name: `pair_block`: every one of the 4 blocks is selected by at least one pair and by at most 12 pairs; one block by exactly 12 pairs.
All inputs are finite; a program needn't handle non-finite values.
Results may differ from a plain program's by a relative error of at most 0.0029.
Values may be sent and summed in bfloat16 or wider, within the bound.
A program may use at most 128 MiB of HBM per device.

v0:
```python
import jax
import jax.numpy as jnp
from jax import lax
from jax.sharding import Mesh
from jax.sharding import PartitionSpec as P

C = 8
V = 8
WROW = ("wrow_0", "wrow_1", "wrow_2")


def from_everyone(array, axis):
    size = lax.axis_size(axis)
    return lax.all_to_all(
        jnp.broadcast_to(array[None], (size, *array.shape)), axis, 0, 0, tiled=True
    )


def laid_out(tiles, dim):
    tiles = jnp.moveaxis(tiles, 0, dim)
    lengths = tiles.shape
    return tiles.reshape(*lengths[:dim], lengths[dim] * lengths[dim + 1], *lengths[dim + 2 :])


def gather_directly(array, axis, dim):
    tiles = from_everyone(array, axis)
    return laid_out(tiles, dim)


def all_blocks(array, axes, order):
    tiles = array[None]
    for k in order:
        tiles = lax.all_gather(tiles, axes[k], axis=0, tiled=True)
    current = [lax.axis_size(axes[k]) for k in reversed(order)]
    tiles = tiles.reshape(*current, *array.shape)
    turned = sorted(range(len(order)), key=lambda place: order[len(order) - 1 - place])
    return tiles.transpose(*turned, *range(len(order), tiles.ndim)).reshape(-1, *array.shape)


def whole_of(array, axes, order, dim):
    return laid_out(all_blocks(array, axes, order), dim)


def split_up(array, dim, size):
    lengths = array.shape
    tiles = array.reshape(*lengths[:dim], size, lengths[dim] // size, *lengths[dim + 1 :])
    return jnp.moveaxis(tiles, dim, 0)


def summed_on_arrival(array, axis, dim):
    size = lax.axis_size(axis)
    tiles = lax.all_to_all(split_up(array, dim, size), axis, 0, 0, tiled=True)
    return jnp.sum(tiles, axis=0)


def per_device(conduction, valence, screened, pair_block):
    gathered_cond = gather_directly(conduction, "kblk", 0)
    gathered_vale = whole_of(valence, WROW, (2, 0, 1), 2)
    k_count = gathered_cond.shape[0]
    kp_count = gathered_cond.shape[1]
    pair_count = k_count * kp_count
    row_width = gathered_cond.shape[3]
    col_width = gathered_vale.shape[3]
    cond_flat = gathered_cond.reshape(pair_count, C * C, row_width)
    vale_flat = gathered_vale.reshape(pair_count, V * V, col_width)
    flat_blocks = pair_block.reshape(pair_count)
    pair_ids = jnp.arange(pair_count, dtype=jnp.int32)
    capacity = 3 * pair_count // 8
    block_count = screened.shape[0]

    def one_block(block, total):
        sort_keys = jnp.where(flat_blocks == block, 0, pair_count) + pair_ids
        chosen = jnp.argsort(sort_keys)[:capacity]
        present = (flat_blocks[chosen] == block).astype(jnp.float32)
        vale_sel = jnp.take(vale_flat, chosen, axis=0)
        cond_sel = jnp.take(cond_flat, chosen, axis=0)
        w_tile = lax.dynamic_index_in_dim(screened, block, 0, keepdims=False)
        screened_vale = jnp.einsum(
            "pvh,gh->pvg", vale_sel, w_tile, preferred_element_type=jnp.float32
        ).astype(jnp.bfloat16)
        tiles = jnp.einsum(
            "pcg,pvg->pcv", cond_sel, screened_vale, preferred_element_type=jnp.float32
        )
        placer = (pair_ids[:, None] == chosen[None, :]).astype(jnp.float32) * present[None, :]
        return total + jnp.einsum("sp,pcv->scv", placer, tiles, precision=lax.Precision.HIGHEST)

    terms = lax.fori_loop(
        0, block_count, one_block, jnp.zeros((pair_count, C * C, V * V), jnp.float32)
    )
    terms = terms.reshape(k_count, kp_count, C, C, V, V).transpose(0, 2, 4, 1, 3, 5)
    terms = terms.reshape(k_count, C * V, kp_count * C * V)
    by_block = summed_on_arrival(terms, "kblk", 0)
    return summed_on_arrival(by_block, WROW, 1)


def solution(mesh):
    finer = Mesh(
        mesh.devices.reshape(4, 4, 2, mesh.shape["kblk"]), ("wrow_0", "wrow_1", "wrow_2", "kblk")
    )
    return jax.shard_map(
        per_device,
        mesh=finer,
        in_specs=(
            P("kblk", None, None, WROW),
            P(None, None, WROW, "kblk"),
            P(None, WROW, "kblk"),
            P(),
        ),
        out_specs=P("kblk", WROW, None),
        check_vma=False,
    )
```

profile of v0, /device:TPU:1, one launch (start us, length us, event | category | flops | bytes accessed | tf_op | source)
XLA Modules:
  0.0 318.4 jit_solution(7045564395566666385)
XLA Ops:
  6.5 0.0 copy-start.2
  6.5 0.0 all-gather.4.cloned.1.call-start
  6.5 1.1 copy.24
  7.7 8.1 %all-gather = bf16[16,4,2,2048]{3,1,2,0:T(4,128)(2,1)S(1)} all-gather(bf16[8,4,2,2048]{3,1,2,0:T(4,128)(2,1)S(1)} %copy.24), channel_id=2, replica_groups=mesh['wrow_0'=4,'wrow_1'=4,'wrow_2'=2,'kblk'=8] {'wrow_2'}, dimensions={0}, use_global_device_ids=true | all-gather | bytes 786432 | tf_op jit(solution)/shard_map/all_gather | solution.py:33
  15.8 1.1 copy.25
  16.9 0.0 all-gather.4.cloned.1.call-update
  16.9 0.0 all-gather.6.cloned.1.call-start
  16.9 37.7 %all-gather.4.cloned.1.call-done = bf16[8,8,4,2,2048]{4,1,3,2,0:T(8,128)(2,1)} async-done(((bf16[2,8,4,2,2048]{4,1,3,2,0:T(8,128)(2,1)}), bf16[8,8,4,2,2048]{4,1,3,2,0:T(8,128)(2,1)}) %all-gather.4.cloned.1.call-update) | async-done | bytes 2097168 | tf_op jit(solution)/shard_map/all_gather | solution.py:33
  54.6 0.0 all-gather.6.cloned.1.call-update
  54.6 0.0 copy-done.2
  54.6 0.0 copy-start.3
  54.7 1.6 broadcast_in_dim.84
  56.3 7.8 %all-to-all-start = ((bf16[8,1,4,64,512]{4,3,2,1,0:T(8,128)(2,1)}), bf16[8,1,4,64,512]{4,3,2,1,0:T(8,128)(2,1)S(1)}, u32[]{:S(2)}, u32[]{:S(2)}) async-start(bf16[8,1,4,64,512]{4,3,2,1,0:T(8,128)(2,1)} %broadcast_in_dim.84), calls=%async_computation | async-start | bytes 4194304 | tf_op jit(solution)/shard_map/all_to_all | solution.py:14
  64.1 0.0 copy-done.3
  64.1 0.1 copy.23
  64.2 0.1 reshape.31
  64.3 77.8 %all-gather.6.cloned.1.call-done = bf16[32,8,4,2,2048]{4,1,3,2,0:T(8,128)(2,1)} async-done(((bf16[8,8,4,2,2048]{4,1,3,2,0:T(8,128)(2,1)}), bf16[32,8,4,2,2048]{4,1,3,2,0:T(8,128)(2,1)}) %all-gather.6.cloned.1.call-update) | async-done | bytes 8388624 | tf_op jit(solution)/shard_map/all_gather | solution.py:33
  142.1 8.3 %copy.26 = bf16[4,4,2,8,4,2,2048]{6,3,5,4,2,1,0:T(8,128)(2,1)} copy(bf16[4,4,2,8,4,2,2048]{6,3,5,4,2,0,1:T(8,128)(2,1)} %bitcast.39) | data formatting | bytes 16777216 | tf_op jit(solution)/shard_map/transpose | solution.py:37
  150.3 16.5 %copy.27 = bf16[8,4,32,2,2048]{4,3,2,1,0:T(2,128)(2,1)} copy(bf16[8,4,32,2,2048]{4,0,3,1,2:T(8,128)(2,1)} %bitcast.36) | data formatting | bytes 16777216 | tf_op jit(solution)/shard_map/transpose | solution.py:20
  166.8 13.1 %reshape_reshape.10 = bf16[32,64,2048]{2,1,0:T(8,128)(2,1)} reshape(bf16[8,4,32,2,2048]{4,3,2,1,0:T(2,128)(2,1)} %copy.27) | data formatting | bytes 16777216 | tf_op jit(solution)/shard_map/reshape;reshape | solution.py:65
  179.9 0.0 all-to-all-done
  179.9 66.1 %while.15 = (s32[]{:T(128)}, f32[32,64,64]{2,0,1:T(8,128)}, s32[32]{0:T(128)S(1)}, bf16[32,64,512]{2,1,0:T(8,128)(2,1)S(1)}, bf16[32,64,2048]{2,1,0:T(8,128)(2,1...) while((s32[]{:T(128)}, f32[32,64,64]{2,0,1:T(8,128)}, s32[32]{0:T(128)S(1)}, ...), condition=%wide.region_2.3_spmd.clone.clone, body=%wide.region_0.2_spmd.clone.clone.sunk | while | flops 1682442368 | bytes 32119912 | solution.py:87
  179.9 1.6 sort.28
  181.5 0.0 copy-done
  181.5 4.1 %gather_fusion = bf16[12,64,2048]{2,1,0:T(8,128)(2,1)S(1)} fusion(bf16[32,64,2048]{2,1,0:T(8,128)(2,1)} %get-tuple-element.254, s32[1024]{0:T(1024)S(1)} %pad_clamp_fusion.2), kind=kCustom, calls=%fused_computation.2.clone.clone.1 | custom fusion | bytes 6291504 | tf_op jit(solution)/shard_map/while/body/eval_jaxpr/jit(_take)/gather | solution.py:75
  185.7 3.1 gather_fusion.1
  188.8 3.9 %fusion.46 = f32[12,64,64]{2,1,0:T(8,128)S(1)} fusion(bf16[4,512,2048]{2,1,0:T(8,128)(2,1)} %get-tuple-element.255, s32[]{:T(128)} %get-tuple-element.242, bf16[12,64,2048]{2,1,0:T(8,128)(2,1)S(1)} %gather_fusion, pred[12]{0:T(512)(128)(4,1)S(1)} %get-tuple-element.233, bf16[12,64,512]{2,1,0:T(8,128)(2,1)} %gather_fusion.1), kind=kOutput, calls=%fused_computation.12.clone.1 | convolution fusion | flops 1663303680 | bytes 6227456 | tf_op jit(solution)/shard_map/while/body/eval_jaxpr/pcg,pvg->pcv/dot_general | solution.py:81
  192.7 0.0 copy-start.1
  192.7 0.7 gather_fusion.2
  193.3 2.2 convolution_add_fusion.2
  195.5 0.0 copy-done.1
  195.5 1.6 sort.28
  197.1 0.0 copy-done
  197.1 4.1 %gather_fusion = bf16[12,64,2048]{2,1,0:T(8,128)(2,1)S(1)} fusion(bf16[32,64,2048]{2,1,0:T(8,128)(2,1)} %get-tuple-element.254, s32[1024]{0:T(1024)S(1)} %pad_clamp_fusion.2), kind=kCustom, calls=%fused_computation.2.clone.clone.1 | custom fusion | bytes 6291504 | tf_op jit(solution)/shard_map/while/body/eval_jaxpr/jit(_take)/gather | solution.py:75
  201.3 3.1 gather_fusion.1
  204.4 3.9 %fusion.46 = f32[12,64,64]{2,1,0:T(8,128)S(1)} fusion(bf16[4,512,2048]{2,1,0:T(8,128)(2,1)} %get-tuple-element.255, s32[]{:T(128)} %get-tuple-element.242, bf16[12,64,2048]{2,1,0:T(8,128)(2,1)S(1)} %gather_fusion, pred[12]{0:T(512)(128)(4,1)S(1)} %get-tuple-element.233, bf16[12,64,512]{2,1,0:T(8,128)(2,1)} %gather_fusion.1), kind=kOutput, calls=%fused_computation.12.clone.1 | convolution fusion | flops 1663303680 | bytes 6227456 | tf_op jit(solution)/shard_map/while/body/eval_jaxpr/pcg,pvg->pcv/dot_general | solution.py:81
  208.3 0.0 copy-start.1
  208.3 0.7 gather_fusion.2
  209.0 3.4 %convolution_add_fusion.2 = f32[32,64,64]{2,0,1:T(8,128)} fusion(f32[32,64,64]{2,0,1:T(8,128)} %get-tuple-element.243, f32[12,64,64]{2,1,0:T(8,128)S(1)} %fusion.46, pred[]{:T(512)S(6)} %compare.7, f32[12]{0:T(128)S(1)} %compare_convert_fusion.2, s32[12]{0:T(128)S(1)} %bitcast.43), kind=kOutput, calls=%fused_computation.11.clone.1 | convolution fusion | flops 19137280 | bytes 1245281 | tf_op jit(solution)/shard_map/while/body/eval_jaxpr/sp,pcv->scv/dot_general | solution.py:85
  212.3 0.0 copy-done.1
  212.4 1.6 sort.28
  214.0 0.0 copy-done
  214.0 4.1 %gather_fusion = bf16[12,64,2048]{2,1,0:T(8,128)(2,1)S(1)} fusion(bf16[32,64,2048]{2,1,0:T(8,128)(2,1)} %get-tuple-element.254, s32[1024]{0:T(1024)S(1)} %pad_clamp_fusion.2), kind=kCustom, calls=%fused_computation.2.clone.clone.1 | custom fusion | bytes 6291504 | tf_op jit(solution)/shard_map/while/body/eval_jaxpr/jit(_take)/gather | solution.py:75
  218.1 3.1 gather_fusion.1
  221.2 3.9 %fusion.46 = f32[12,64,64]{2,1,0:T(8,128)S(1)} fusion(bf16[4,512,2048]{2,1,0:T(8,128)(2,1)} %get-tuple-element.255, s32[]{:T(128)} %get-tuple-element.242, bf16[12,64,2048]{2,1,0:T(8,128)(2,1)S(1)} %gather_fusion, pred[12]{0:T(512)(128)(4,1)S(1)} %get-tuple-element.233, bf16[12,64,512]{2,1,0:T(8,128)(2,1)} %gather_fusion.1), kind=kOutput, calls=%fused_computation.12.clone.1 | convolution fusion | flops 1663303680 | bytes 6227456 | tf_op jit(solution)/shard_map/while/body/eval_jaxpr/pcg,pvg->pcv/dot_general | solution.py:81
  225.1 0.0 copy-start.1
  225.1 0.7 gather_fusion.2
  225.8 3.4 %convolution_add_fusion.2 = f32[32,64,64]{2,0,1:T(8,128)} fusion(f32[32,64,64]{2,0,1:T(8,128)} %get-tuple-element.243, f32[12,64,64]{2,1,0:T(8,128)S(1)} %fusion.46, pred[]{:T(512)S(6)} %compare.7, f32[12]{0:T(128)S(1)} %compare_convert_fusion.2, s32[12]{0:T(128)S(1)} %bitcast.43), kind=kOutput, calls=%fused_computation.11.clone.1 | convolution fusion | flops 19137280 | bytes 1245281 | tf_op jit(solution)/shard_map/while/body/eval_jaxpr/sp,pcv->scv/dot_general | solution.py:85
  229.2 0.0 copy-done.1
  229.2 1.6 sort.28
  230.8 0.0 copy-done
  230.8 4.1 %gather_fusion = bf16[12,64,2048]{2,1,0:T(8,128)(2,1)S(1)} fusion(bf16[32,64,2048]{2,1,0:T(8,128)(2,1)} %get-tuple-element.254, s32[1024]{0:T(1024)S(1)} %pad_clamp_fusion.2), kind=kCustom, calls=%fused_computation.2.clone.clone.1 | custom fusion | bytes 6291504 | tf_op jit(solution)/shard_map/while/body/eval_jaxpr/jit(_take)/gather | solution.py:75
  234.9 3.1 gather_fusion.1
  238.0 3.9 %fusion.46 = f32[12,64,64]{2,1,0:T(8,128)S(1)} fusion(bf16[4,512,2048]{2,1,0:T(8,128)(2,1)} %get-tuple-element.255, s32[]{:T(128)} %get-tuple-element.242, bf16[12,64,2048]{2,1,0:T(8,128)(2,1)S(1)} %gather_fusion, pred[12]{0:T(512)(128)(4,1)S(1)} %get-tuple-element.233, bf16[12,64,512]{2,1,0:T(8,128)(2,1)} %gather_fusion.1), kind=kOutput, calls=%fused_computation.12.clone.1 | convolution fusion | flops 1663303680 | bytes 6227456 | tf_op jit(solution)/shard_map/while/body/eval_jaxpr/pcg,pvg->pcv/dot_general | solution.py:81
  241.9 0.0 copy-start.1
  242.0 0.7 gather_fusion.2
  242.6 3.4 %convolution_add_fusion.2 = f32[32,64,64]{2,0,1:T(8,128)} fusion(f32[32,64,64]{2,0,1:T(8,128)} %get-tuple-element.243, f32[12,64,64]{2,1,0:T(8,128)S(1)} %fusion.46, pred[]{:T(512)S(6)} %compare.7, f32[12]{0:T(128)S(1)} %compare_convert_fusion.2, s32[12]{0:T(128)S(1)} %bitcast.43), kind=kOutput, calls=%fused_computation.11.clone.1 | convolution fusion | flops 19137280 | bytes 1245281 | tf_op jit(solution)/shard_map/while/body/eval_jaxpr/sp,pcv->scv/dot_general | solution.py:85
  246.0 0.0 copy-done.1
  246.0 5.9 %reshape.34 = f32[8,4,8,8,8,8]{5,4,1,0,3,2:T(8,128)} reshape(f32[32,64,64]{2,0,1:T(8,128)} %get-tuple-element.133) | data formatting | bytes 1048576 | tf_op jit(solution)/shard_map/reshape | solution.py:90
  252.0 14.7 %copy.33 = f32[8,4,8,8,8,8]{5,3,1,4,2,0:T(8,128)} copy(f32[8,4,8,8,8,8]{5,4,1,0,3,2:T(8,128)} %reshape.34) | data formatting | bytes 1048576 | tf_op jit(solution)/shard_map/reshape | solution.py:90
  266.6 6.9 %reshape_reshape.11 = f32[8,1,64,256]{3,2,0,1:T(8,128)S(1)} reshape(f32[8,8,8,4,8,8]{5,4,3,2,1,0:T(8,128)} %bitcast.37) | data formatting | bytes 1048576 | tf_op jit(solution)/shard_map/reshape;reshape | solution.py:46
  273.6 23.7 %all_to_all.15 = f32[8,1,64,256]{3,2,1,0:T(8,128)S(1)} all-to-all(f32[8,1,64,256]{3,2,1,0:T(8,128)S(1)} %bitcast.40), channel_id=1, replica_groups=mesh['wrow_0'=4,'wrow_1'=4,'wrow_2'=2,'kblk'=8] {'kblk'}, dimensions={0} | all-to-all | bytes 1048576 | tf_op jit(solution)/shard_map/all_to_all | solution.py:52
  297.4 13.5 %all_to_all.16 = f32[32,1,2,256]{3,2,1,0:T(2,128)S(1)} all-to-all(f32[32,1,2,256]{3,2,1,0:T(2,128)S(1)} %transpose_reshape.3), channel_id=1, replica_groups=mesh['wrow_0'=4,'wrow_1'=4,'wrow_2'=2,'kblk'=8] {'wrow_0','wrow_1','wrow..., dimensions={0} | all-to-all | bytes 131072 | tf_op jit(solution)/shard_map/all_to_all | solution.py:52
  310.9 0.6 reduce_sum.21
  (27 shorter events, 0.2 us)
Async XLA Ops:
  6.5 48.1 %copy-start.2 = (bf16[1,4,64,512]{3,2,1,0:T(8,128)(2,1)S(1)}, bf16[1,4,64,512]{3,2,1,0:T(8,128)(2,1)}, u32[]{:S(2)}) copy-start(bf16[1,4,64,512]{3,2,1,0:T(8,128)(2,1)} %param.6) | copy-start | bytes 786436
  6.5 48.1 %all-gather.4.cloned.1.call-start = ((), (), s32[]{:S(2)}) async-start(), calls=%async_computation.3 | async-start | bytes 2621440 | tf_op jit(solution)/shard_map/all_gather | solution.py:33
  16.9 125.2 %all-gather.6.cloned.1.call-start = ((), (), s32[]{:S(2)}) async-start(), calls=%async_computation.4 | async-start | bytes 10485760 | tf_op jit(solution)/shard_map/all_gather | solution.py:33
  54.6 9.5 %copy-start.3 = (s32[8,4]{0,1:T(4,128)S(1)}, s32[8,4]{0,1:T(4,128)}, u32[]{:S(2)}) copy-start(s32[8,4]{0,1:T(4,128)} %param.9) | copy-start | bytes 388
  56.3 123.6 %all-to-all-start = ((bf16[8,1,4,64,512]{4,3,2,1,0:T(8,128)(2,1)}), bf16[8,1,4,64,512]{4,3,2,1,0:T(8,128)(2,1)S(1)}, u32[]{:S(2)}, u32[]{:S(2)}) async-start(bf16[8,1,4,64,512]{4,3,2,1,0:T(8,128)(2,1)} %broadcast_in_dim.84), calls=%async_computation | async-start | bytes 4194304 | tf_op jit(solution)/shard_map/all_to_all | solution.py:14
  179.9 1.6 copy-start
  192.7 2.8 copy-start.1
  195.5 1.6 copy-start
  208.3 4.1 %copy-start.1 = (bf16[32,64,512]{2,1,0:T(8,128)(2,1)S(1)}, bf16[32,64,512]{2,1,0:T(8,128)(2,1)}, u32[]{:S(2)}) copy-start(bf16[32,64,512]{2,1,0:T(8,128)(2,1)} %copy-done) | copy-start | bytes 6291460 | tf_op jit(solution)/shard_map/while
  212.3 1.6 copy-start
  225.1 4.1 %copy-start.1 = (bf16[32,64,512]{2,1,0:T(8,128)(2,1)S(1)}, bf16[32,64,512]{2,1,0:T(8,128)(2,1)}, u32[]{:S(2)}) copy-start(bf16[32,64,512]{2,1,0:T(8,128)(2,1)} %copy-done) | copy-start | bytes 6291460 | tf_op jit(solution)/shard_map/while
  229.2 1.6 copy-start
  241.9 4.1 %copy-start.1 = (bf16[32,64,512]{2,1,0:T(8,128)(2,1)S(1)}, bf16[32,64,512]{2,1,0:T(8,128)(2,1)}, u32[]{:S(2)}) copy-start(bf16[32,64,512]{2,1,0:T(8,128)(2,1)} %copy-done) | copy-start | bytes 6291460 | tf_op jit(solution)/shard_map/while
Sparse Core Ops, SparseCore 0:
  17.0 37.5 all-gather.3
  56.4 85.6 all-gather.5
where the time goes:
time: 320 us; the launch traced here: 318 us
  waiting for transfers between devices  115 us (36%)
  local copies, waits for them, and re-layouts  101 us (32%)
  blocking collectives  45.3 us (14%)
  matrix products  27.9 us (9%)
  between operations  13.4 us (4%)
  starting transfers between devices  7.89 us (2%)
  other arithmetic  7.06 us (2%)
    all_gather x2, waiting for transfers between devices, all_blocks(): tiles = lax.all_gather(tiles, axes[k], axis=0, tiled=True)  115 us
    all_to_all x2, blocking collectives, summed_on_arrival(): tiles = lax.all_to_all(split_up(array, dim, size), axis, 0, 0, tiled=True)  37.2 us
    reshape x2, local copies, waits for them, and re-layouts, per_device(): terms.reshape(k_count, kp_count, C, C, V, V).transpose(0, 2, 4, 1, 3, 5)  20.6 us
    gather x4, local copies, waits for them, and re-layouts, one_block(): vale_sel = jnp.take(vale_flat, chosen, axis=0)  16.5 us
    transpose x1, local copies, waits for them, and re-layouts, laid_out(): tiles = jnp.moveaxis(tiles, 0, dim)  16.5 us
    dot_general x4, matrix products, one_block(): jnp.einsum('pcg,pvg->pcv', cond_sel, screened_vale, preferred_element_typ...  15.6 us
    another operation x1, local copies, waits for them, and re-layouts, per_device(): vale_flat = gathered_vale.reshape(pair_count, V * V, col_width)  13.1 us
    gather x4, local copies, waits for them, and re-layouts, one_block(): cond_sel = jnp.take(cond_flat, chosen, axis=0)  12.4 us
  transfers between devices with their start and end apart: 3, of which 2 were waited for; matrix products, arithmetic and copies ran while one was open for 12% of the time, Pallas kernels for 0%

commit v1 on v0

v1 whole, which is shorter than its diff:
```python
import functools

import jax
import jax.numpy as jnp
from jax import lax
from jax.experimental import pallas as pl
from jax.experimental.pallas import tpu as pltpu
from jax.sharding import Mesh
from jax.sharding import PartitionSpec as P

AXES = ("py", "px", "zl", "zh", "core")
WROW = ("py", "px", "zl")
KBLK = ("zh", "core")
MESH = pl.DeviceIdType.MESH
DMA = pltpu.SemaphoreType.DMA


def kernel(vale, cond, screened, ql, out,
           vbuf, cbuf, wbuf, xacc, xhold, zs, zrecv, total, r1buf, t1, r2buf,
           lsem, ssem, rsem, cssem, crsem, dsem, r1s, r1r, r2s, r2r):
    py, px, zl, zh, core = (lax.axis_index(a) for a in AXES)
    me = dict(py=py, px=px, zl=zl, zh=zh, core=core)

    def at(**moved):
        return tuple(moved.get(a, me[a]) for a in AXES)

    def mod4(v):
        return lax.rem(v + 8, 4)

    own_k = zh * 2 + core
    first = ("px", "py")
    second = ("py", "px")

    def slot(h, d1, d2, zz):
        return (h, mod4(me[second[h]] + d2), mod4(me[first[h]] + d1), lax.rem(zl + zz, 2))

    locals_ = []
    for h in range(2):
        locals_.append(pltpu.make_async_copy(vale.at[h], vbuf.at[slot(h, 0, 0, 0)], lsem.at[h]))
    locals_.append(pltpu.make_async_copy(cond, cbuf.at[own_k], lsem.at[2]))
    locals_.append(pltpu.make_async_copy(screened, wbuf, lsem.at[3]))
    for c in locals_:
        c.start()

    barrier = pltpu.get_barrier_semaphore()
    for dy in range(4):
        for dx in range(4):
            if dx or dy:
                pl.semaphore_signal(barrier, inc=1, device_id=at(py=mod4(py + dy), px=mod4(px + dx)),
                                    device_id_type=MESH)
    for dl in range(2):
        for dh in range(4):
            for dc in range(2):
                if dl or dh or dc:
                    pl.semaphore_signal(
                        barrier, inc=1,
                        device_id=at(zl=lax.rem(zl + dl, 2), zh=mod4(zh + dh), core=lax.rem(core + dc, 2)),
                        device_id_type=MESH)
    for c in locals_[:3]:
        c.wait()
    pl.semaphore_wait(barrier, 30)

    started = []

    def send(src, dst, s, r, to):
        c = pltpu.make_async_remote_copy(src_ref=src, dst_ref=dst, send_sem=s, recv_sem=r,
                                         device_id=to, device_id_type=MESH)
        c.start()
        started.append(c)

    counts = [0, 0]

    def vsend(h, chunk, axis, step):
        d1, d2, zz = chunk
        ref = vbuf.at[slot(h, d1, d2, zz)]
        if axis == "zl":
            to, r = at(zl=1 - zl), (h, 0, 0, 1)
        else:
            to = at(**{axis: mod4(me[axis] + step)})
            r = ((h, d2 % 4, (d1 - step) % 4, zz) if axis == first[h] else (h, (d2 - step) % 4, d1 % 4, zz))
        send(ref, ref, ssem.at[h, counts[h]], rsem.at[r], to)
        counts[h] += 1

    def vwait(h, chunk):
        d1, d2, zz = chunk
        ref = vbuf.at[slot(h, d1, d2, zz)]
        sem = rsem.at[h, d2 % 4, d1 % 4, zz]
        pltpu.make_async_remote_copy(src_ref=ref, dst_ref=ref, send_sem=sem, recv_sem=sem,
                                     device_id=at(core=1 - core), device_id_type=MESH).wait_recv()

    def phase1(h, chunk):
        d1, _, zz = chunk
        if d1 == 0:
            vsend(h, chunk, first[h], 1)
            vsend(h, chunk, first[h], -1)
        if d1 == -1 and zz == 0:
            vsend(h, chunk, first[h], 1)
        if d1 == 1 and zz == 1:
            vsend(h, chunk, first[h], -1)

    def phase2(h, chunk):
        vsend(h, chunk, second[h], 1)
        vsend(h, chunk, second[h], -1)

    def csend(o):
        send(cbuf.at[own_k], cbuf.at[own_k], cssem.at[o], crsem.at[o], at(zh=mod4(zh + o)))

    def partner(o):
        ref = cbuf.at[mod4(zh - o) * 2 + core]
        send(ref, ref, cssem.at[4 + o], crsem.at[4 + o], at(core=1 - core))

    def cwait(o, far):
        ref = cbuf.at[mod4(zh - o) * 2 + (1 - core if far else core)]
        sem = crsem.at[(4 if far else 0) + o]
        pltpu.make_async_remote_copy(src_ref=ref, dst_ref=ref, send_sem=sem, recv_sem=sem,
                                     device_id=at(core=1 - core), device_id_type=MESH).wait_recv()

    own = (0, 0, 0)
    for h in range(2):
        vsend(h, own, "zl", 1)
    for h in range(2):
        phase1(h, own)
    partner(0)
    for h in range(2):
        phase2(h, own)
    for o in (1, 3, 2):
        csend(o)

    for chunks in (((0, 0, 1),), ((-1, 0, 0), (1, 0, 0)), ((-1, 0, 1), (1, 0, 1)), ((2, 0, 0), (2, 0, 1))):
        for chunk in chunks:
            for h in range(2):
                vwait(h, chunk)
                phase1(h, chunk)
                phase2(h, chunk)
    locals_[3].wait()

    lane = lax.broadcasted_iota(jnp.int32, (64, 256), 1)
    pair_of_lane = lax.rem(lax.div(lane, 2), 16)

    def stage1(h, d2):
        a2 = mod4(me[second[h]] + d2)
        block_of_lane = ql[h][0:1]

        @pl.loop(0, 4)
        def _(q):
            v = vbuf[h, a2].reshape(256, 2048)
            x = lax.dot_general(wbuf[q], v, (((1,), (1,)), ((), ())), preferred_element_type=jnp.float32)
            chosen = jnp.broadcast_to(block_of_lane == q, x.shape)
            xacc[...] = jnp.where(jnp.logical_or(chosen, q == 0), x, xacc[...])

    def stage2(h, d2, x):
        a2 = mod4(me[second[h]] + d2)
        z = jnp.zeros((64, 256), jnp.float32)
        for kk in range(4):
            y = jnp.dot(cbuf[4 * h + kk].reshape(256, 512), x, preferred_element_type=jnp.float32)
            for kp in range(4):
                z = jnp.where(pair_of_lane == kk * 4 + kp, y[kp * 64:kp * 64 + 64], z)
        for half in range(2):
            tile = z[:, half * 128:half * 128 + 128].reshape(8, 8, 128)
            if h == 0:
                zs[0, lax.div(a2, 2), :, lax.rem(a2, 2) * 2 + half] = tile
            else:
                zs[1, half, :, a2] = tile

    for h in range(2):
        stage1(h, 0)
        xhold[h] = xacc[...].astype(jnp.bfloat16)

    def forward(d1):
        for zz in range(2):
            for h in range(2):
                for d2 in (-1, 1):
                    chunk = (d1, d2, zz)
                    vwait(h, chunk)
                    if d2 == -1 and zz == 0:
                        vsend(h, chunk, second[h], 1)
                    if d2 == 1 and zz == 1:
                        vsend(h, chunk, second[h], -1)

    forward(0)
    cwait(0, True)
    for o in (1, 3, 2):
        cwait(o, False)
        partner(o)
    for o in (1, 3, 2):
        cwait(o, True)
    forward(-1)
    for h in range(2):
        stage2(h, 0, xhold[h])
    for d1 in (1, 2):
        forward(d1)
    for d2 in (-1, 1):
        for h in range(2):
            stage1(h, d2)
            stage2(h, d2, xacc[...].astype(jnp.bfloat16))
    for h in range(2):
        for d1 in (0, -1, 1, 2):
            for zz in range(2):
                vwait(h, (d1, 2, zz))
        stage1(h, 2)
        stage2(h, 2, xacc[...].astype(jnp.bfloat16))

    send(zs.at[1 - core], zrecv, dsem.at[0], dsem.at[1], at(core=1 - core))
    started.pop().wait()
    total[...] = zs[core] + zrecv[...]

    offsets = [(dy, dx) for dy in range(4) for dx in range(4) if dx or dy]
    for dy, dx in offsets:
        ty, tx = mod4(py + dy), mod4(px + dx)
        i = dy * 4 + dx
        send(total.at[lax.rem(tx, 2), ty * 2 + lax.div(tx, 2)], r1buf.at[i], r1s.at[i], r1r.at[i], at(py=ty, px=tx))
    acc = total[lax.rem(px, 2), py * 2 + lax.div(px, 2)]
    for dy, dx in offsets:
        i = dy * 4 + dx
        pltpu.make_async_remote_copy(src_ref=r1buf.at[i], dst_ref=r1buf.at[i], send_sem=r1s.at[i], recv_sem=r1r.at[i],
                                     device_id=at(core=1 - core), device_id_type=MESH).wait_recv()
        acc = acc + r1buf[i]
    t1[...] = acc

    here = zl * 4 + zh
    for tl in range(2):
        for th in range(2):
            for tc in range(2):
                i = tl * 4 + th * 2 + tc
                dest = at(zl=tl, zh=core * 2 + th, core=tc)
                mine = jnp.logical_and(jnp.logical_and(zl == tl, core == tc), zh == core * 2 + th)
                copy = pltpu.make_async_remote_copy(src_ref=t1, dst_ref=r2buf.at[here], send_sem=r2s.at[i],
                                                    recv_sem=r2r.at[here], device_id=dest, device_id_type=MESH)

                @pl.when(jnp.logical_not(mine))
                def _():
                    copy.start()

                @pl.when(mine)
                def _():
                    r2buf[here] = acc

    for i in range(8):
        mine = jnp.logical_and(lax.div(zh, 2) == core, here == i)

        @pl.when(jnp.logical_not(mine))
        def _():
            pltpu.make_async_remote_copy(src_ref=t1, dst_ref=r2buf.at[i], send_sem=r2s.at[i], recv_sem=r2r.at[i],
                                         device_id=at(core=1 - core), device_id_type=MESH).wait_recv()

    acc = r2buf[0]
    for i in range(1, 8):
        acc = acc + r2buf[i]
    out[...] = acc

    for c in started:
        c.wait_send()
    for tl in range(2):
        for th in range(2):
            for tc in range(2):
                i = tl * 4 + th * 2 + tc
                mine = jnp.logical_and(jnp.logical_and(zl == tl, core == tc), zh == core * 2 + th)

                @pl.when(jnp.logical_not(mine))
                def _():
                    pltpu.make_async_remote_copy(src_ref=t1, dst_ref=t1, send_sem=r2s.at[i], recv_sem=r2r.at[i],
                                                 device_id=at(core=1 - core), device_id_type=MESH).wait_send()


def per_device(conduction, valence, screened, pair_block):
    vale = valence.reshape(2, 32, 2048)
    cond = conduction.reshape(4, 64, 512)
    pairs = pair_block.reshape(2, 1, 1, 16, 1)
    ql = jnp.broadcast_to(pairs, (2, 8, 8, 16, 2)).reshape(2, 8, 256)
    part = pl.pallas_call(
        kernel,
        out_shape=jax.ShapeDtypeStruct((4, 8, 128), jnp.float32),
        in_specs=[pl.BlockSpec(memory_space=pl.ANY)] * 3 + [pl.BlockSpec(memory_space=pltpu.VMEM)],
        out_specs=pl.BlockSpec(memory_space=pltpu.VMEM),
        scratch_shapes=[
            pltpu.VMEM((2, 4, 4, 2, 32, 2048), jnp.bfloat16),
            pltpu.VMEM((8, 4, 64, 512), jnp.bfloat16),
            pltpu.VMEM((4, 512, 2048), jnp.bfloat16),
            pltpu.VMEM((512, 256), jnp.float32),
            pltpu.VMEM((2, 512, 256), jnp.bfloat16),
            pltpu.VMEM((2, 2, 8, 4, 8, 128), jnp.float32),
            pltpu.VMEM((2, 8, 4, 8, 128), jnp.float32),
            pltpu.VMEM((2, 8, 4, 8, 128), jnp.float32),
            pltpu.VMEM((16, 4, 8, 128), jnp.float32),
            pltpu.VMEM((4, 8, 128), jnp.float32),
            pltpu.VMEM((8, 4, 8, 128), jnp.float32),
            DMA((4,)),
            DMA((2, 31)),
            DMA((2, 4, 4, 2)),
            DMA((8,)),
            DMA((8,)),
            DMA((2,)),
            DMA((16,)),
            DMA((16,)),
            DMA((8,)),
            DMA((8,)),
        ],
        compiler_params=pltpu.CompilerParams(collective_id=0, has_side_effects=True,
                                             vmem_limit_bytes=48 * 1024 * 1024),
    )(vale, cond, screened, ql)
    zl, zh, core = (lax.axis_index(a) for a in ("zl", "zh", "core"))
    kk = lax.rem(zh, 2) * 2 + core
    lo = part.reshape(2, 2, 8, 2, 2, 4, 4, 2)
    lo = lax.dynamic_index_in_dim(lo, zl, 0, False)
    lo = lax.dynamic_index_in_dim(lo, kk, 4, False)
    lo = lo.transpose(0, 4, 1, 2, 3, 5)
    hi = part.reshape(2, 2, 8, 2, 2, 4, 4, 2)
    hi = lax.dynamic_index_in_dim(hi, zl, 3, False)
    hi = lax.dynamic_index_in_dim(hi, kk, 4, False)
    hi = hi.transpose(0, 4, 2, 1, 3, 5)
    return jnp.where(zh < 2, lo.reshape(1, 2, 256), hi.reshape(1, 2, 256))


def solution(mesh):
    finer = Mesh(mesh.devices.reshape(4, 4, 2, 4, 2), AXES)
    return jax.shard_map(
        per_device,
        mesh=finer,
        in_specs=(P(KBLK, None, None, WROW), P(None, None, WROW, KBLK), P(None, WROW, KBLK), P()),
        out_specs=P(KBLK, WROW, None),
        check_vma=False,
    )
```

time: 320 us -> 93.2 us (0.29)
  waiting for transfers between devices: 115 us -> 0 us
  local copies, waits for them, and re-layouts: 101 us -> 4.25 us
  Pallas kernels: 0 us -> 88.7 us
  blocking collectives: 45.3 us -> 0 us
  matrix products: 27.9 us -> 0 us
  between operations: 13.4 us -> 0.06 us
  starting transfers between devices: 7.89 us -> 0 us
  other arithmetic: 7.06 us -> 0.02 us
    all_gather x2 -> x0, waiting for transfers between devices: 115 us -> none  [all_blocks(): tiles = lax.all_gather(tiles, axes[k], axis=0, tiled=True)]
    pallas_call x0 -> x1, Pallas kernels: none -> 88.7 us  [per_device(): pl.pallas_call(kernel, out_shape=jax.ShapeDtypeStruct((4, 8, 128), jnp.fl...]
    all_to_all x2 -> x0, blocking collectives: 37.2 us -> none  [summed_on_arrival(): tiles = lax.all_to_all(split_up(array, dim, size), axis, 0, 0, tiled=True)]
    gather x12 -> x0, local copies, waits for them, and re-layouts: 31.6 us -> none  [the longest x4 16.5 us: one_block(): vale_sel = jnp.take(vale_flat, chosen, axis=0)]
    dot_general x8 -> x0, matrix products: 27.9 us -> none  [the longest x4 15.6 us: one_block(): jnp.einsum('pcg,pvg->pcv', cond_sel, screened_vale, preferred_element_typ...]
    transpose x2 -> x0, local copies, waits for them, and re-layouts: 24.7 us -> none  [the longest x1 16.5 us: laid_out(): tiles = jnp.moveaxis(tiles, 0, dim)]
    another operation x3 -> x0, local copies, waits for them, and re-layouts: 20.1 us -> none  [the longest x1 13.1 us: per_device(): vale_flat = gathered_vale.reshape(pair_count, V * V, col_width)]
    reshape x3 -> x1, local copies, waits for them, and re-layouts: 20.7 us -> 1.05 us  [per_device(): vale = valence.reshape(2, 32, 2048)]
  transfers between devices with their start and end apart: 3 -> 0, of which waited for: 2 -> 0; matrix products, arithmetic and copies ran while one was open for 12% -> 0% of each run, Pallas kernels for 0% -> 0%
where the time goes in v1:
time: 93.2 us; the launch traced here: 93 us
  Pallas kernels  88.7 us (95%)
  local copies, waits for them, and re-layouts  4.25 us (5%)
    pallas_call x1, Pallas kernels, per_device(): pl.pallas_call(kernel, out_shape=jax.ShapeDtypeStruct((4, 8, 128), jnp.fl...  88.7 us

profile of v1, /device:TPU:1, one launch (start us, length us, event | category | flops | bytes accessed | tf_op | source)
XLA Modules:
  0.0 93.0 jit_solution(5461758812270655197)
XLA Ops:
  0.0 0.8 copy.6
  0.8 0.1 broadcast_in_dim.11
  0.8 0.1 broadcast_in_dim.12
  0.9 0.1 broadcast_in_dim.13
  1.1 1.1 %reshape.44.vale = bf16[2,32,2048]{2,1,0:T(8,128)(2,1)S(1)} reshape(bf16[8,4,2,2048]{3,2,1,0:T(2,128)(2,1)} %param.5) | data formatting | bytes 524288 | tf_op jit(solution)/shard_map/reshape | solution.py:266
  2.1 0.0 copy-start
  2.1 0.9 %copy-done = bf16[1,4,64,512]{3,2,1,0:T(8,128)(2,1)S(1)} copy-done((bf16[1,4,64,512]{3,2,1,0:T(8,128)(2,1)S(1)}, bf16[1,4,64,512]{3,2,1,0:T(8,128)(2,1)}, u32[]{:S(2)}) %copy-start) | copy-done | bytes 262168
  3.1 88.7 %shard_map.46 = f32[4,8,128]{2,1,0:T(8,128)S(1)} custom-call(bf16[2,32,2048]{2,1,0:T(8,128)(2,1)S(1)} %reshape.44.vale, bf16[4,64,512]{2,1,0:T(8,128)(2,1)S(1)} %bitcast.12, bf16[4,512,2048]{2,1,0:T(8,128)(2,1)} %screened.1, s32[2,8,256]{2,1,0:T(8,128)S(1)} %broadcast_in_dim.14.ql), custom_call_target="tpu_custom_call" | custom-call | tf_op jit(solution)/shard_map/pallas_call | solution.py:270
  91.8 0.1 copy.7
  92.0 0.3 copy.10
  92.3 0.8 select_n.41
  (4 shorter events, 0.1 us)
Async XLA Ops:
  2.1 1.0 %copy-start = (bf16[1,4,64,512]{3,2,1,0:T(8,128)(2,1)S(1)}, bf16[1,4,64,512]{3,2,1,0:T(8,128)(2,1)}, u32[]{:S(2)}) copy-start(bf16[1,4,64,512]{3,2,1,0:T(8,128)(2,1)} %param.4) | copy-start | bytes 786436
